TPU v7x, 32 devices: a whole 2x2x4 slice. The times are simulated.
32 devices in a mesh: freq: 16 (over z, x, core), grid: 2 (over y).
Axes of the slice: x: 2, y: 2, z: 4, core: 2. Of those that a mesh axis runs over, the one named last changes fastest.
Arguments:
- cross_spectra: float32 [2, 32, 256, 256], P(None, None, 'freq', 'grid'), as said below
- sensor_modes: float32 [32, 96, 256], P('freq', None, 'grid'), may hold values from -0.375 to 0.375
- source_modes: float32 [32, 96, 256], P('freq', None, 'grid'), may hold values from -6 to 6
- wavenumber: float32 [32, 96], P('freq'), may hold values from 0.5 to 2
- attenuation: float32 [32, 96], P('freq'), may hold values from 0.002 to 0.03
- mode_counts: int32 [32], P('freq'), may hold values from 48 to 96
Outputs:
- bartlett_power: float32 [64, 256], P('freq', 'grid')
Inputs may be any that keep to these rules, and one draw needn't show every extreme that they name: `cross_spectra`: each bin's matrix K_f is Hermitian and positive definite. Modes with index mode_counts[f] or more are left out in bin f.
All inputs are finite; a program needn't handle non-finite values.
Results may differ from a plain program's by a relative error of at most 0.0003.
Values sent between devices are 32-bit elements; how exact they have to be, the bound alone decides.
A program may use at most 128 MiB of HBM per device.

v0:
```python
import functools

import jax
import jax.numpy as jnp
from jax import lax
from jax.experimental import pallas as pl
from jax.experimental.pallas import tpu as pltpu
from jax.sharding import PartitionSpec as P

RANGES = 64
BLOCK = 8
STEP = 8
LANES = 128

HIGH = lax.Precision.HIGHEST
MESH = pl.DeviceIdType.MESH
NT = (((1,), (1,)), ((), ()))
NN = (((1,), (0,)), ((), ()))


def split(value):
    high = value.astype(jnp.bfloat16)
    return high, (value - high.astype(jnp.float32)).astype(jnp.bfloat16)


def product(left, right, dims):
    return lax.dot_general(left, right, dims, preferred_element_type=jnp.float32)


def kernel(
    nf, ng,
    spectra_hbm, sensor_hbm, source_hbm, wave_ref, atten_ref, counts_ref,
    out_ref,
    raw, outgoing, table, shapes, sources, shapes_wide, halves, weight, rows_scr, cols_scr, row_in,
    u_scr, v_scr, lhs, denom, power, parts,
    raw_sem, own_sem, mode_send, mode_recv, send_sem, recv_sem, part_send, part_recv,
):
    devices = nf * ng
    bins = outgoing.shape[0]
    nb = bins // devices
    row_count, col_count = raw.shape[2], raw.shape[3]
    modes = shapes.shape[2]
    ranges = u_scr.shape[1]
    share = ranges // nf
    depth_here = sources.shape[3]
    my_f, my_g = lax.axis_index("freq"), lax.axis_index("grid")
    me = my_f * ng + my_g

    raw_copy = pltpu.make_async_copy(spectra_hbm, raw, raw_sem)
    raw_copy.start()
    own = pl.ds(my_g * nb, nb)
    own_shapes = pltpu.make_async_copy(sensor_hbm.at[own], shapes.at[my_g], own_sem.at[0])
    own_sources = pltpu.make_async_copy(source_hbm.at[own], sources.at[my_g], own_sem.at[1])
    own_shapes.start()
    own_sources.start()

    barrier = pltpu.get_barrier_semaphore()

    def greet(k, carry):
        peer = lax.rem(me + k, devices)
        pl.semaphore_signal(
            barrier, inc=1, device_id=(peer // ng, lax.rem(peer, ng)), device_id_type=MESH
        )
        return carry

    lax.fori_loop(1, devices, greet, 0)

    raw_copy.wait()
    outgoing[...] = raw[0] + raw[1]
    my_rows = pl.ds(pl.multiple_of(my_f * row_count, row_count), row_count)
    for b in range(nb):
        table[my_g, b, my_rows, :] = outgoing[me * nb + b]

    pl.semaphore_wait(barrier, devices - 1)

    def mode_copies(k):
        peer = lax.rem(my_g + k, ng)
        theirs = pl.ds(peer * nb, nb)
        return [
            pltpu.make_async_remote_copy(
                src_ref=hbm.at[theirs],
                dst_ref=here.at[my_g],
                send_sem=mode_send.at[i, k],
                recv_sem=mode_recv.at[i, k],
                device_id=(my_f, peer),
                device_id_type=MESH,
            )
            for i, (hbm, here) in enumerate(((sensor_hbm, shapes), (source_hbm, sources)))
        ]

    for k in range(1, ng):
        for copy in mode_copies(k):
            copy.start()

    def piece(k):
        peer = lax.rem(me + k, devices)
        return pltpu.make_async_remote_copy(
            src_ref=outgoing.at[pl.ds(peer * nb, nb)],
            dst_ref=table.at[my_g, :, my_rows, :],
            send_sem=send_sem.at[k],
            recv_sem=recv_sem.at[k],
            device_id=(peer // ng, lax.rem(peer, ng)),
            device_id_type=MESH,
        )

    def send_piece(k, carry):
        piece(k).start()
        return carry

    lax.fori_loop(1, devices, lambda k, c: send_piece(devices - k, c), 0)

    for b in range(nb):
        row = my_g * nb + b
        row_in[...] = jnp.ones_like(row_in)
        row_in[0:1, 0:modes] = wave_ref[pl.ds(row, 1), :]
        row_in[1:2, 0:modes] = atten_ref[pl.ds(row, 1), :]
        radius = 1.0 + lax.broadcasted_iota(jnp.int32, (ranges, LANES), 0).astype(jnp.float32)
        lane = lax.broadcasted_iota(jnp.int32, (ranges, LANES), 1)
        phase = radius * row_in[0:1, :]
        magnitude = jnp.exp(-row_in[1:2, :] * radius) / jnp.sqrt(phase)
        magnitude = jnp.where(lane < counts_ref[row], magnitude, 0.0)
        filler = jnp.zeros((LANES - ranges, LANES), jnp.float32)
        for i, factor in enumerate((magnitude * jnp.cos(phase), magnitude * jnp.sin(phase))):
            rows_scr[b, i] = factor
            turned = jnp.concatenate([factor, filler], 0).T
            for blk in range(ranges // BLOCK):
                cols_scr[b, i, blk] = turned[0:modes, blk * BLOCK : (blk + 1) * BLOCK]

    for b in range(nb):

        def pair_block(blk, carry):
            first = pl.multiple_of(blk * BLOCK, BLOCK)
            row_real = rows_scr[b, 0, pl.ds(first, BLOCK), :]
            row_imag = rows_scr[b, 1, pl.ds(first, BLOCK), :]
            col_real, col_imag = cols_scr[b, 0, blk], cols_scr[b, 1, blk]
            for k in range(BLOCK):
                nr, ni = row_real[k : k + 1, :], row_imag[k : k + 1, :]
                mr = jnp.broadcast_to(col_real[:, k : k + 1], (modes, LANES))
                mi = jnp.broadcast_to(col_imag[:, k : k + 1], (modes, LANES))
                u_scr[b, first + k] = mr * nr + mi * ni
                v_scr[b, first + k] = mr * ni - mi * nr
            return carry

        lax.fori_loop(0, ranges // BLOCK, pair_block, 0)

    own_shapes.wait()
    own_sources.wait()
    for k in range(1, ng):
        for copy in mode_copies(k):
            copy.wait_recv()

    shapes_wide[...] = jnp.zeros_like(shapes_wide)
    halves[...] = jnp.zeros_like(halves)
    for b in range(nb):
        for g in range(ng):
            shapes_wide[b, 0:modes, g * col_count : (g + 1) * col_count] = shapes[g, b]
            exact = sources[g, b]
            rounded = exact.astype(jnp.bfloat16)
            at = slice(g * depth_here, (g + 1) * depth_here)
            halves[b, 0:modes, at] = rounded
            halves[b, LANES : LANES + modes, at] = rounded
            weight[b, :, at] = 2.0 * exact - rounded.astype(jnp.float32)

    def put(i, k, block):
        high = block.astype(jnp.bfloat16)
        low = (block - high.astype(jnp.float32)).astype(jnp.bfloat16)
        lhs[i, k * modes : (k + 1) * modes, 0:LANES] = high
        lhs[i, k * modes : (k + 1) * modes, LANES : 2 * LANES] = low

    def forms(i, b):
        image = jnp.dot(lhs[i], halves[b], preferred_element_type=jnp.float32)
        image = image.reshape(BLOCK, modes, image.shape[1]) * weight[b][None]
        return jnp.sum(image, axis=1)

    for b in range(nb):
        wide = shapes_wide[b]
        gram = lax.dot_general(
            wide[0:modes], wide, NT, precision=HIGH, preferred_element_type=jnp.float32
        )

        def denom_step(step, carry):
            for i in range(STEP):
                first = pl.multiple_of((step * STEP + i) * BLOCK, BLOCK)
                for k in range(BLOCK):
                    put(i, k, gram * u_scr[b, first + k])
                denom[b, pl.ds(first, BLOCK), :] = forms(i, b) * float(bins)
            return carry

        lax.fori_loop(0, ranges // BLOCK // STEP, denom_step, 0)

    def part(peer, slot):
        peer_f, peer_g = peer // ng, lax.rem(peer, ng)
        return pltpu.make_async_remote_copy(
            src_ref=power.at[peer_g, peer_f],
            dst_ref=parts.at[slot],
            send_sem=part_send.at[peer],
            recv_sem=part_recv.at[slot],
            device_id=(peer_f, peer_g),
            device_id_type=MESH,
        )

    blocks = ranges // BLOCK
    owners = BLOCK // share
    low = 1 - (my_f // owners * 2) // blocks

    def block_at(n):
        return lax.rem(my_f // owners + (1 - 2 * low) * (n + 1) + blocks, blocks)

    def send_block(n):
        for t in range(owners):
            for g in range(ng):
                part((block_at(n) * owners + t) * ng + g, me).start()

    def take_piece(k, carry):
        piece(k).wait_recv()
        return carry

    lax.fori_loop(1, devices, take_piece, 0)

    for b in range(nb):
        wide = shapes_wide[b]
        whole = jnp.concatenate([table[g, b] for g in range(ng)], axis=1)
        left_high, left_low = split(wide)
        mid_high, mid_low = split(whole)
        both = jnp.concatenate([left_high, left_low], 0)
        half = product(both, mid_high, NN)
        half = half[:LANES] + (half[LANES:] + product(left_high, mid_low, NN))
        half_high, half_low = split(half)
        both = jnp.concatenate([half_high, half_low], 0)
        full = product(both, left_high, NT)
        full = full[:LANES] + (full[LANES:] + product(half_high, left_low, NT))
        turned = full.T
        even = (0.5 * (full + turned))[0:modes]
        odd = (0.5 * (full - turned))[0:modes]

        def numer_step(step, carry):
            for i in range(STEP):
                blk = block_at(step * STEP + i)
                first = pl.multiple_of(blk * BLOCK, BLOCK)
                for k in range(BLOCK):
                    put(i, k, even * u_scr[b, first + k] - odd * v_scr[b, first + k])
                score = forms(i, b) / denom[b, pl.ds(first, BLOCK), :]
                for g in range(ng):
                    for t in range(owners):
                        at = slice(g * depth_here, (g + 1) * depth_here)
                        value = score[t * share : (t + 1) * share, at]
                        slot = blk * owners + t
                        if b == 0:
                            power[g, slot] = value
                        else:
                            power[g, slot] += value
                if b == nb - 1 and i > 0:
                    send_block(step * STEP + i - 1)
                elif b == nb - 1:

                    @pl.when(step > 0)
                    def _():
                        send_block(step * STEP - 1)

            return carry

        lax.fori_loop(0, ranges // BLOCK // STEP, numer_step, 0)

    def send_last(k, carry):
        peer = me // (owners * ng) * (owners * ng) + lax.rem(me + k, owners * ng)
        part(peer, me).start()
        return carry

    lax.fori_loop(1, owners * ng, send_last, 0)
    parts[me] = power[my_g, my_f]

    def finish(k, carry):
        piece(k).wait_send()
        peer = lax.rem(me + k, devices)
        part(peer, me).wait_send()
        part(peer, peer).wait_recv()
        return carry

    for k in range(1, ng):
        for copy in mode_copies(k):
            copy.wait_send()
    lax.fori_loop(1, devices, finish, 0)
    out_ref[...] = jnp.sum(parts[...], axis=0)


def solution(mesh):
    nf, ng = mesh.shape["freq"], mesh.shape["grid"]
    devices = nf * ng

    def per_device(cross_spectra, sensor_modes, source_modes, wavenumber, attenuation, mode_counts):
        two, bins, rows, cols = cross_spectra.shape
        bins_here, modes, _ = sensor_modes.shape
        depth_here = source_modes.shape[2]
        nb = bins_here // ng
        ranges = RANGES // nf * nf
        share = ranges // nf
        f32, bf16 = jnp.float32, jnp.bfloat16
        dma = pltpu.SemaphoreType.DMA
        return pl.pallas_call(
            functools.partial(kernel, nf, ng),
            out_shape=jax.ShapeDtypeStruct((share, depth_here), f32),
            in_specs=[pl.BlockSpec(memory_space=pl.ANY)] * 3
            + [pl.BlockSpec(memory_space=pltpu.VMEM)] * 2
            + [pl.BlockSpec(memory_space=pltpu.SMEM)],
            out_specs=pl.BlockSpec(memory_space=pltpu.VMEM),
            scratch_shapes=[
                pltpu.VMEM((two, bins, rows, cols), f32),
                pltpu.VMEM((bins, rows, cols), f32),
                pltpu.VMEM((ng, nb, nf * rows, cols), f32),
                pltpu.VMEM((ng, nb, modes, cols), f32),
                pltpu.VMEM((ng, nb, modes, depth_here), f32),
                pltpu.VMEM((nb, LANES, ng * cols), f32),
                pltpu.VMEM((nb, 2 * LANES, ng * depth_here), bf16),
                pltpu.VMEM((nb, modes, ng * depth_here), f32),
                pltpu.VMEM((nb, 2, ranges, LANES), f32),
                pltpu.VMEM((nb, 2, ranges // BLOCK, modes, BLOCK), f32),
                pltpu.VMEM((8, LANES), f32),
                pltpu.VMEM((nb, ranges, modes, LANES), f32),
                pltpu.VMEM((nb, ranges, modes, LANES), f32),
                pltpu.VMEM((STEP, BLOCK * modes, 2 * LANES), bf16),
                pltpu.VMEM((nb, ranges, ng * depth_here), f32),
                pltpu.VMEM((ng, nf, share, depth_here), f32),
                pltpu.VMEM((devices, share, depth_here), f32),
                dma, dma((2,)), dma((2, ng)), dma((2, ng)),
                dma((devices,)), dma((devices,)), dma((devices,)), dma((devices,)),
            ],
            compiler_params=pltpu.CompilerParams(
                collective_id=0, has_side_effects=True, vmem_limit_bytes=60 * 1024 * 1024
            ),
        )(cross_spectra, sensor_modes, source_modes, wavenumber, attenuation, mode_counts)

    placed = (
        P(None, None, "freq", "grid"),
        P("freq", None, "grid"),
        P("freq", None, "grid"),
        P("freq", None),
        P("freq", None),
        P("freq"),
    )
    return jax.shard_map(
        per_device, mesh=mesh, in_specs=placed, out_specs=P("freq", "grid"), check_vma=False
    )
```

profile of v0, /device:TPU:0, one launch (start us, length us, event | category | flops | bytes accessed | tf_op | source)
XLA Modules:
  0.0 25.4 jit_solution(2453478127714008832)
XLA Ops:
  0.0 24.2 %shard_map.64 = f32[4,128]{1,0:T(4,128)} custom-call(f32[2,32,16,128]{3,2,1,0:T(8,128)} %spectra_hbm.1, f32[2,96,128]{2,1,0:T(8,128)} %sensor_hbm.1, f32[2,96,128]{2,1,0:T(8,128)} %source_hbm.1, f32[2,96]{1,0:T(2,128)} %wave_ref.1, f32[2,96]{1,0:T(2,128)} %atten_ref.1, s32[2]{0:T(128)} %counts_ref.1), custom_call_target="tpu_custom_call" | custom-call | tf_op jit(solution)/shard_map/pallas_call | solution.py:299
  24.2 1.3 %copy.8 = f32[4,128]{1,0:T(4,128)} copy(f32[4,128]{1,0:T(4,128)} %shard_map.64) | data formatting | bytes 4096
where the time goes:
time: 25.6 us; the launch traced here: 25.4 us
  Pallas kernels  24.2 us (95%)
  local copies, waits for them, and re-layouts  1.26 us (5%)
    pallas_call x1, Pallas kernels, per_device(): pl.pallas_call(functools.partial(kernel, nf, ng), out_shape=jax.ShapeDtyp...  24.2 us
    unnamed x1, local copies, waits for them, and re-layouts  1.26 us

commit v1 on v0

--- a/solution.py
+++ b/solution.py
@@ -29,8 +29,9 @@
 
 def kernel(
     nf, ng,
-    spectra_hbm, sensor_hbm, source_hbm, wave_ref, atten_ref, counts_ref,
+    spectra_hbm, sensor_hbm, source_hbm, wave_hbm, atten_hbm, counts_hbm,
     out_ref,
+    wave_ref, atten_ref, counts_ref, small_sem,
     raw, outgoing, table, shapes, sources, shapes_wide, halves, weight, rows_scr, cols_scr, row_in,
     u_scr, v_scr, lhs, denom, power, parts,
     raw_sem, own_sem, mode_send, mode_recv, send_sem, recv_sem, part_send, part_recv,
@@ -48,6 +49,14 @@
 
     raw_copy = pltpu.make_async_copy(spectra_hbm, raw, raw_sem)
     raw_copy.start()
+    small = [
+        pltpu.make_async_copy(hbm, here, small_sem.at[i])
+        for i, (hbm, here) in enumerate(
+            ((wave_hbm, wave_ref), (atten_hbm, atten_ref), (counts_hbm, counts_ref))
+        )
+    ]
+    for copy in small:
+        copy.start()
     own = pl.ds(my_g * nb, nb)
     own_shapes = pltpu.make_async_copy(sensor_hbm.at[own], shapes.at[my_g], own_sem.at[0])
     own_sources = pltpu.make_async_copy(source_hbm.at[own], sources.at[my_g], own_sem.at[1])
@@ -66,6 +75,8 @@
     lax.fori_loop(1, devices, greet, 0)
 
     raw_copy.wait()
+    for copy in small:
+        copy.wait()
     outgoing[...] = raw[0] + raw[1]
     my_rows = pl.ds(pl.multiple_of(my_f * row_count, row_count), row_count)
     for b in range(nb):
@@ -97,8 +108,8 @@
         return pltpu.make_async_remote_copy(
             src_ref=outgoing.at[pl.ds(peer * nb, nb)],
             dst_ref=table.at[my_g, :, my_rows, :],
-            send_sem=send_sem.at[k],
-            recv_sem=recv_sem.at[k],
+            send_sem=send_sem,
+            recv_sem=recv_sem,
             device_id=(peer // ng, lax.rem(peer, ng)),
             device_id_type=MESH,
         )
@@ -193,8 +204,8 @@
         return pltpu.make_async_remote_copy(
             src_ref=power.at[peer_g, peer_f],
             dst_ref=parts.at[slot],
-            send_sem=part_send.at[peer],
-            recv_sem=part_recv.at[slot],
+            send_sem=part_send,
+            recv_sem=part_recv,
             device_id=(peer_f, peer_g),
             device_id_type=MESH,
         )
@@ -215,7 +226,11 @@
         piece(k).wait_recv()
         return carry
 
-    lax.fori_loop(1, devices, take_piece, 0)
+    many = outgoing.at[pl.ds(0, (devices - 1) * nb)]
+    most = parts.at[pl.ds(0, devices - 1)]
+    def settle(ref, sem):
+        pltpu.make_async_copy(ref, ref, sem).wait()
+    settle(many, recv_sem)
 
     for b in range(nb):
         wide = shapes_wide[b]
@@ -269,17 +284,13 @@
     lax.fori_loop(1, owners * ng, send_last, 0)
     parts[me] = power[my_g, my_f]
 
-    def finish(k, carry):
-        piece(k).wait_send()
-        peer = lax.rem(me + k, devices)
-        part(peer, me).wait_send()
-        part(peer, peer).wait_recv()
-        return carry
 
     for k in range(1, ng):
         for copy in mode_copies(k):
             copy.wait_send()
-    lax.fori_loop(1, devices, finish, 0)
+    settle(many, send_sem)
+    settle(most, part_send)
+    settle(most, part_recv)
     out_ref[...] = jnp.sum(parts[...], axis=0)
 
 
@@ -299,11 +310,10 @@
         return pl.pallas_call(
             functools.partial(kernel, nf, ng),
             out_shape=jax.ShapeDtypeStruct((share, depth_here), f32),
-            in_specs=[pl.BlockSpec(memory_space=pl.ANY)] * 3
-            + [pl.BlockSpec(memory_space=pltpu.VMEM)] * 2
-            + [pl.BlockSpec(memory_space=pltpu.SMEM)],
+            in_specs=[pl.BlockSpec(memory_space=pltpu.HBM)] * 6,
             out_specs=pl.BlockSpec(memory_space=pltpu.VMEM),
             scratch_shapes=[
+                pltpu.VMEM(wavenumber.shape, f32), pltpu.VMEM(attenuation.shape, f32), pltpu.SMEM(mode_counts.shape, jnp.int32), pltpu.SemaphoreType.DMA((3,)),
                 pltpu.VMEM((two, bins, rows, cols), f32),
                 pltpu.VMEM((bins, rows, cols), f32),
                 pltpu.VMEM((ng, nb, nf * rows, cols), f32),
@@ -322,12 +332,12 @@
                 pltpu.VMEM((ng, nf, share, depth_here), f32),
                 pltpu.VMEM((devices, share, depth_here), f32),
                 dma, dma((2,)), dma((2, ng)), dma((2, ng)),
-                dma((devices,)), dma((devices,)), dma((devices,)), dma((devices,)),
+                dma, dma, dma, dma,
             ],
             compiler_params=pltpu.CompilerParams(
-                collective_id=0, has_side_effects=True, vmem_limit_bytes=60 * 1024 * 1024
+                collective_id=0, has_side_effects=True, vmem_limit_bytes=24 * 1024 * 1024
             ),
-        )(cross_spectra, sensor_modes, source_modes, wavenumber, attenuation, mode_counts)
+        )(*[pltpu.with_memory_space_constraint(x, pltpu.HBM) for x in (cross_spectra, sensor_modes, source_modes, wavenumber, attenuation, mode_counts)])
 
     placed = (
         P(None, None, "freq", "grid"),

time: 25.6 us -> 21.9 us (0.86)
  Pallas kernels: 24.2 us -> 21.1 us
  local copies, waits for them, and re-layouts: 1.26 us -> 0.58 us
    pallas_call x1, Pallas kernels: 24.2 us -> 21.1 us  [per_device(): pl.pallas_call(functools.partial(kernel, nf, ng), out_shape=jax.ShapeDtyp...]
    unnamed x1, local copies, waits for them, and re-layouts: 1.26 us -> 0.58 us
where the time goes in v1:
time: 21.9 us; the launch traced here: 21.7 us
  Pallas kernels  21.1 us (96%)
  local copies, waits for them, and re-layouts  0.58 us (3%)
    pallas_call x1, Pallas kernels, per_device(): pl.pallas_call(functools.partial(kernel, nf, ng), out_shape=jax.ShapeDtyp...  21.1 us
    unnamed x1, local copies, waits for them, and re-layouts  0.58 us

profile of v1, /device:TPU:0, one launch (start us, length us, event | category | flops | bytes accessed | tf_op | source)
XLA Modules:
  0.0 21.7 jit_solution(1434548638765714276)
XLA Ops:
  0.0 21.1 %shard_map.64 = f32[4,128]{1,0:T(4,128)S(1)} custom-call(f32[2,32,16,128]{3,2,1,0:T(8,128)} %spectra_hbm.1, f32[2,96,128]{2,1,0:T(8,128)} %sensor_hbm.1, f32[2,96,128]{2,1,0:T(8,128)} %source_hbm.1, f32[2,96]{1,0:T(2,128)} %wave_hbm.1, f32[2,96]{1,0:T(2,128)} %atten_hbm.1, s32[2]{0:T(128)} %counts_hbm.1), custom_call_target="tpu_custom_call" | custom-call | tf_op jit(solution)/shard_map/pallas_call | solution.py:310
  21.1 0.6 %copy.8 = f32[4,128]{1,0:T(4,128)} copy(f32[4,128]{1,0:T(4,128)S(1)} %shard_map.64) | data formatting | bytes 4096

commit v2 on v1

v2 whole, which is shorter than its diff:
```python
import functools

import jax
import jax.numpy as jnp
from jax import lax
from jax.experimental import pallas as pl
from jax.experimental.pallas import tpu as pltpu
from jax.sharding import PartitionSpec as P

RANGES = 64
LANES = 128
CHUNK = 2
PLANES = 4

HIGH = lax.Precision.HIGHEST
MESH = pl.DeviceIdType.MESH
NT = (((1,), (1,)), ((), ()))
NN = (((1,), (0,)), ((), ()))


def split(value):
    high = value.astype(jnp.bfloat16)
    return high, (value - high.astype(jnp.float32)).astype(jnp.bfloat16)


def product(left, right, dims):
    return lax.dot_general(left, right, dims, preferred_element_type=jnp.float32)


def diagonals(square, modes):
    lane = lax.broadcasted_iota(jnp.int32, square.shape, 1)
    step = 1
    while step < modes:
        turned = pltpu.roll(square, modes - step, 0)
        square = jnp.where(lax.rem(lane // step, 2) == 1, turned, square)
        step *= 2
    return square


def kernel(
    nf, ng,
    spectra_hbm, sensor_hbm, source_hbm, wave_hbm, atten_hbm, counts_hbm,
    out_ref,
    wave, atten, counts, raw, plus, table, modes_out, shapes, sources, wide,
    first, second, right, rows, denom, power, parts,
    known, small_sem, raw_sem, own_sem, mode_send, mode_recv, send_sem, recv_sem, part_send, part_recv,
):
    devices = nf * ng
    bins, row_count, col_count = plus.shape
    nb = bins // devices
    modes = shapes.shape[2]
    half = modes // 2
    ranges = first.shape[2]
    share = ranges // nf
    depth_here = sources.shape[3]
    my_f, my_g = lax.axis_index("freq"), lax.axis_index("grid")
    me = my_f * ng + my_g

    barrier = pltpu.get_barrier_semaphore()
    span = nf // PLANES
    plane = my_f // span

    def flips(index, size):
        deltas, weight = [], 1
        while weight < size:
            deltas.append((1 - 2 * lax.rem(index // weight, 2)) * weight)
            weight *= 2
        return deltas

    flip_f, flip_g = flips(my_f, nf), flips(my_g, ng)

    def flipped(j):
        f, g = my_f, my_g
        for bit, delta in enumerate(flip_g + flip_f):
            if j >> bit & 1:
                if bit < len(flip_g):
                    g = g + delta
                else:
                    f = f + delta
        return f, g

    def signal(semaphore, f, g):
        pl.semaphore_signal(semaphore, inc=1, device_id=(f, g), device_id_type=MESH)

    def greet(f, carry):
        for g in range(ng):
            signal(barrier, nf + (plane + 1) * span - 1 - f, g)
        return carry

    lax.fori_loop((plane + 1) * span, nf, greet, 0)
    for j in range(span * ng - 1, 0, -1):
        signal(barrier, *flipped(j))

    raw_copy = pltpu.make_async_copy(spectra_hbm, raw, raw_sem)
    raw_copy.start()
    small = [
        pltpu.make_async_copy(hbm, here, small_sem.at[i])
        for i, (hbm, here) in enumerate(((wave_hbm, wave), (atten_hbm, atten), (counts_hbm, counts)))
    ]
    own = pl.ds(my_g * nb, nb)
    owned = [
        pltpu.make_async_copy(hbm, here, own_sem.at[i])
        for i, (hbm, here) in enumerate((
            (sensor_hbm, modes_out.at[0]),
            (source_hbm, modes_out.at[1]),
            (sensor_hbm.at[own], shapes.at[my_g]),
            (source_hbm.at[own], sources.at[my_g, :, 0:modes, :]),
            (source_hbm.at[own], sources.at[my_g, :, modes : 2 * modes, :]),
        ))
    ]
    for copy in small + owned:
        copy.start()

    raw_copy.wait()
    plus[...] = raw[0] + raw[1]
    my_rows = pl.ds(pl.multiple_of(my_f * row_count, row_count), row_count)
    for b in range(nb):
        table[my_g, b, my_rows, :] = plus[me * nb + b]

    for copy in owned:
        copy.wait()
    pl.semaphore_wait(barrier, (plane + 1) * span * ng - 1)
    for k in range(PLANES - 1, 0, -1):

        @pl.when(plane >= k)
        def _():
            signal(known.at[plane], my_f - k * span, my_g)

    def mode_copies(k):
        peer = lax.rem(my_g + k, ng)
        theirs = pl.ds(peer * nb, nb)
        places = (shapes.at[my_g], sources.at[my_g, :, 0:modes, :])
        return [
            pltpu.make_async_remote_copy(
                src_ref=modes_out.at[i, theirs],
                dst_ref=here,
                send_sem=mode_send.at[i, k - 1],
                recv_sem=mode_recv.at[i, k - 1],
                device_id=(my_f, peer),
                device_id_type=MESH,
            )
            for i, here in enumerate(places)
        ]

    for k in range(1, ng):
        for copy in mode_copies(k):
            copy.start()

    def piece(f, g):
        return pltpu.make_async_remote_copy(
            src_ref=plus.at[pl.ds((f * ng + g) * nb, nb)],
            dst_ref=table.at[my_g, :, my_rows, :],
            send_sem=send_sem,
            recv_sem=recv_sem,
            device_id=(f, g),
            device_id_type=MESH,
        )

    def send_plane(shift):
        for j in range(span * ng - 1, -1, -1):
            if j > 0 or shift is not None:
                f, g = flipped(j)
                piece(f if shift is None else f + shift, g).start()

    send_plane(None)
    for k in range(PLANES - 1, 0, -1):

        @pl.when(plane >= k)
        def _():
            send_plane(-k * span)

    for copy in small:
        copy.wait()
    radius = 1.0 + lax.broadcasted_iota(jnp.int32, (ranges, LANES), 0).astype(jnp.float32)
    lane = lax.broadcasted_iota(jnp.int32, (ranges, LANES), 1)
    for b in range(nb):
        row = my_g * nb + b
        rows[...] = jnp.ones_like(rows)
        rows[0:1, 0:modes] = wave[pl.ds(row, 1), :]
        rows[1:2, 0:modes] = atten[pl.ds(row, 1), :]
        phase = radius * rows[0:1, :]
        magnitude = jnp.exp(-rows[1:2, :] * radius) / jnp.sqrt(phase)
        magnitude = jnp.where(lane < jnp.minimum(counts[row], modes), magnitude, 0.0)
        first[b, 0] = magnitude * jnp.cos(phase)
        second[b, 0] = magnitude * jnp.sin(phase)

    for b in range(nb):
        real, imag = first[b, 0], second[b, 0]
        ahead = []
        for value in (real + imag, real - imag):
            ahead.append(jnp.where(lane < modes, value, pltpu.roll(value, modes, 1)))
        for d in range(half + 1):
            turned = []
            for value in ahead:
                if d > 0:
                    near = pltpu.roll(value, LANES - d, 1)
                    if modes - 1 + d >= LANES:
                        far = pltpu.roll(value, modes - d, 1)
                        near = jnp.where(lane < LANES - d, near, far)
                    value = near
                turned.append(value)
            total, gap = turned
            one = real * gap + imag * total
            two = real * total - imag * gap
            if d == 0 or 2 * d == modes:
                one, two = 0.5 * one, 0.5 * two
            first[b, d] = one
            second[b, d] = two

    for k in range(1, PLANES):

        @pl.when(plane + k < PLANES)
        def _():
            pl.semaphore_wait(known.at[plane + k], 1)
            send_plane(k * span)

    def lay_products(b, g):
        here = sources[g, b, 0:modes, :]
        none = jnp.zeros((LANES - modes, depth_here), jnp.bfloat16)
        for d in range(half + 1):
            pair = here * sources[g, b, d : d + modes, :]
            high, low = split(pair)
            slots = [(0, high), (1, high), (2, low)] if d == 0 else [(d + 2, high)]
            for slot, value in slots:
                right[b, g, slot * LANES : slot * LANES + modes, :] = value
                if modes < LANES:
                    right[b, g, slot * LANES + modes : (slot + 1) * LANES, :] = none

    for k in range(1, ng):
        for copy in mode_copies(k):
            copy.wait_recv()

    wide[...] = jnp.zeros_like(wide)
    for b in range(nb):
        for g in range(ng):
            wide[b, 0:modes, g * col_count : (g + 1) * col_count] = shapes[g, b]

            @pl.when(my_g != g)
            def _():
                sources[g, b, modes : 2 * modes, :] = sources[g, b, 0:modes, :]

            lay_products(b, g)

    def forms(b, lefts):
        slots = []
        for d in range(half + 1):
            value = lefts(d)
            high, low = split(value)
            slots += [high, low, high] if d == 0 else [high]
        totals = [None] * ng
        for k in range(0, len(slots), CHUNK):
            left = jnp.concatenate(slots[k : k + CHUNK], axis=1)
            end = k + len(slots[k : k + CHUNK])
            for n in range(ng):
                part = product(left, right[b, n, k * LANES : end * LANES, :], NN)
                totals[n] = part if totals[n] is None else totals[n] + part
        return jnp.concatenate(totals, axis=1)

    def spread(ref, d):
        return jnp.broadcast_to(ref[d : d + 1, :], (ranges, LANES))

    for b in range(nb):
        gram = lax.dot_general(
            wide[b, 0:modes], wide[b], NT, precision=HIGH, preferred_element_type=jnp.float32
        )
        rows[0:modes, :] = diagonals(gram, modes)
        value = forms(b, lambda d: spread(rows, d) * (first[b, d] + second[b, d]))
        denom[b] = value * float(bins)

    def settle(ref, sem):
        pltpu.make_async_copy(ref, ref, sem).wait()

    settle(plus.at[pl.ds(0, (devices - 1) * nb)], recv_sem)

    for b in range(nb):
        left_high, left_low = split(wide[b])
        whole = jnp.concatenate([table[g, b] for g in range(ng)], axis=1)
        mid_high, mid_low = split(whole)
        high, low = left_high[0:modes], left_low[0:modes]
        both = product(jnp.concatenate([high, low], 0), mid_high, NN)
        middle = both[:modes] + (both[modes:] + product(high, mid_low, NN))
        half_high, half_low = split(middle)
        both = product(jnp.concatenate([half_high, half_low], 0), left_high, NT)
        forward = both[:modes] + (both[modes:] + product(half_high, left_low, NT))
        square = jnp.zeros((LANES - modes, LANES), jnp.float32)
        backward = jnp.concatenate([forward, square], 0).T[0:modes]
        rows[0:modes, :] = diagonals(backward, modes)
        rows[LANES : LANES + modes, :] = diagonals(forward, modes)

        def left(d):
            return spread(rows, d) * first[b, d] + spread(rows, LANES + d) * second[b, d]

        score = forms(b, left) / denom[b]
        for g in range(ng):
            at = slice(g * depth_here, (g + 1) * depth_here)
            value = score[:, at].reshape(nf, share, depth_here)
            power[g] = value if b == 0 else power[g] + value

    def part(f, g):
        return pltpu.make_async_remote_copy(
            src_ref=power.at[g, f],
            dst_ref=parts.at[me],
            send_sem=part_send,
            recv_sem=part_recv,
            device_id=(f, g),
            device_id_type=MESH,
        )

    for j in range(devices - 1, 0, -1):
        part(*flipped(j)).start()
    parts[me] = power[my_g, my_f]

    for k in range(1, ng):
        for copy in mode_copies(k):
            copy.wait_send()

    settle(plus.at[pl.ds(0, (devices - 1) * nb)], send_sem)
    settle(parts.at[pl.ds(0, devices - 1)], part_send)
    settle(parts.at[pl.ds(0, devices - 1)], part_recv)
    out_ref[...] = jnp.sum(parts[...], axis=0)


def solution(mesh):
    nf, ng = mesh.shape["freq"], mesh.shape["grid"]
    devices = nf * ng

    def per_device(cross_spectra, sensor_modes, source_modes, wavenumber, attenuation, mode_counts):
        two, bins, rows, cols = cross_spectra.shape
        bins_here, modes, _ = sensor_modes.shape
        depth_here = source_modes.shape[2]
        nb = bins_here // ng
        ranges = RANGES // nf * nf
        share = ranges // nf
        slots = modes // 2 + 3
        f32, bf16 = jnp.float32, jnp.bfloat16
        dma = pltpu.SemaphoreType.DMA
        operands = (
            cross_spectra, sensor_modes, source_modes, wavenumber, attenuation, mode_counts
        )
        return pl.pallas_call(
            functools.partial(kernel, nf, ng),
            out_shape=jax.ShapeDtypeStruct((share, depth_here), f32),
            in_specs=[pl.BlockSpec(memory_space=pltpu.HBM)] * 6,
            out_specs=pl.BlockSpec(memory_space=pltpu.VMEM),
            scratch_shapes=[
                pltpu.VMEM((bins_here, modes), f32),
                pltpu.VMEM((bins_here, modes), f32),
                pltpu.SMEM((bins_here,), jnp.int32),
                pltpu.VMEM((two, bins, rows, cols), f32),
                pltpu.VMEM((bins, rows, cols), f32),
                pltpu.VMEM((ng, nb, nf * rows, cols), f32),
                pltpu.VMEM((2, bins_here, modes, cols), f32),
                pltpu.VMEM((ng, nb, modes, cols), f32),
                pltpu.VMEM((ng, nb, 2 * modes, depth_here), f32),
                pltpu.VMEM((nb, LANES, ng * cols), f32),
                pltpu.VMEM((nb, modes // 2 + 1, ranges, LANES), f32),
                pltpu.VMEM((nb, modes // 2 + 1, ranges, LANES), f32),
                pltpu.VMEM((nb, ng, slots * LANES, depth_here), bf16),
                pltpu.VMEM((2 * LANES, LANES), f32),
                pltpu.VMEM((nb, ranges, ng * depth_here), f32),
                pltpu.VMEM((ng, nf, share, depth_here), f32),
                pltpu.VMEM((devices, share, depth_here), f32),
                pltpu.SemaphoreType.REGULAR((PLANES,)),
                dma((3,)), dma, dma((5,)), dma((2, max(ng - 1, 1))), dma((2, max(ng - 1, 1))),
                dma, dma, dma, dma,
            ],
            compiler_params=pltpu.CompilerParams(
                collective_id=0, has_side_effects=True, vmem_limit_bytes=32 * 1024 * 1024
            ),
        )(*[pltpu.with_memory_space_constraint(x, pltpu.HBM) for x in operands])

    placed = (
        P(None, None, "freq", "grid"),
        P("freq", None, "grid"),
        P("freq", None, "grid"),
        P("freq", None),
        P("freq", None),
        P("freq"),
    )
    return jax.shard_map(
        per_device, mesh=mesh, in_specs=placed, out_specs=P("freq", "grid"), check_vma=False
    )
```

time: 21.9 us -> 20.9 us (0.954)
  Pallas kernels: 21.1 us -> 20.2 us
    pallas_call x1, Pallas kernels: 21.1 us -> 20.2 us  [per_device(): pl.pallas_call(functools.partial(kernel, nf, ng), out_shape=jax.ShapeDtyp...]
where the time goes in v2:
time: 20.9 us; the launch traced here: 20.8 us
  Pallas kernels  20.2 us (97%)
  local copies, waits for them, and re-layouts  0.58 us (3%)
    pallas_call x1, Pallas kernels, per_device(): pl.pallas_call(functools.partial(kernel, nf, ng), out_shape=jax.ShapeDtyp...  20.2 us
    unnamed x1, local copies, waits for them, and re-layouts  0.58 us

profile of v2, /device:TPU:0, one launch (start us, length us, event | category | flops | bytes accessed | tf_op | source)
XLA Modules:
  0.0 20.8 jit_solution(56197705520327023)
XLA Ops:
  0.0 20.2 %shard_map.64 = f32[4,128]{1,0:T(4,128)S(1)} custom-call(f32[2,32,16,128]{3,2,1,0:T(8,128)} %spectra_hbm.1, f32[2,96,128]{2,1,0:T(8,128)} %sensor_hbm.1, f32[2,96,128]{2,1,0:T(8,128)} %source_hbm.1, f32[2,96]{1,0:T(2,128)} %wave_hbm.1, f32[2,96]{1,0:T(2,128)} %atten_hbm.1, s32[2]{0:T(128)} %counts_hbm.1), custom_call_target="tpu_custom_call" | custom-call | tf_op jit(solution)/shard_map/pallas_call | solution.py:340
  20.2 0.6 %copy.8 = f32[4,128]{1,0:T(4,128)} copy(f32[4,128]{1,0:T(4,128)S(1)} %shard_map.64) | data formatting | bytes 4096

commit v3 on v2

--- a/solution.py
+++ b/solution.py
@@ -25,6 +25,12 @@
 
 def product(left, right, dims):
     return lax.dot_general(left, right, dims, preferred_element_type=jnp.float32)
+
+
+def thrice(left, right, rows, dims):
+    high, low = left[0][0:rows], left[1][0:rows]
+    both = product(jnp.concatenate([high, low], 0), right[0], dims)
+    return both[:rows] + (both[rows:] + product(high, right[1], dims))
 
 
 def diagonals(square, modes):
@@ -41,20 +47,26 @@
     nf, ng,
     spectra_hbm, sensor_hbm, source_hbm, wave_hbm, atten_hbm, counts_hbm,
     out_ref,
-    wave, atten, counts, raw, plus, table, modes_out, shapes, sources, wide,
+    wave, atten, counts, raw, plus, minus, table, mirror, relay, modes_out, shapes, sources,
     first, second, right, rows, denom, power, parts,
-    known, small_sem, raw_sem, own_sem, mode_send, mode_recv, send_sem, recv_sem, part_send, part_recv,
+    known, small_sem, raw_sem, own_sem, mode_send, mode_recv, send_sem, recv_sem,
+    relay_send, relay_recv, part_send, part_recv,
 ):
     devices = nf * ng
-    bins, row_count, col_count = plus.shape
-    nb = bins // devices
-    modes = shapes.shape[2]
+    nb, row_count, col_count = plus.shape[2:]
+    paired = ng == 2
+    per = nf // ng
+    group = per * row_count
+    modes = modes_out.shape[2]
     half = modes // 2
     ranges = first.shape[2]
     share = ranges // nf
     depth_here = sources.shape[3]
     my_f, my_g = lax.axis_index("freq"), lax.axis_index("grid")
     me = my_f * ng + my_g
+    home = my_f // per
+    crossed = home != my_g
+    straight = home == my_g
 
     barrier = pltpu.get_barrier_semaphore()
     span = nf // PLANES
@@ -103,7 +115,7 @@
         for i, (hbm, here) in enumerate((
             (sensor_hbm, modes_out.at[0]),
             (source_hbm, modes_out.at[1]),
-            (sensor_hbm.at[own], shapes.at[my_g]),
+            (sensor_hbm.at[own], shapes.at[my_g, :, 0:modes, :]),
             (source_hbm.at[own], sources.at[my_g, :, 0:modes, :]),
             (source_hbm.at[own], sources.at[my_g, :, modes : 2 * modes, :]),
         ))
@@ -112,10 +124,28 @@
         copy.start()
 
     raw_copy.wait()
-    plus[...] = raw[0] + raw[1]
+    plus[...] = (raw[0] + raw[1]).reshape(plus.shape)
     my_rows = pl.ds(pl.multiple_of(my_f * row_count, row_count), row_count)
+    near_rows = pl.ds(pl.multiple_of(lax.rem(my_f, per) * row_count, row_count), row_count)
     for b in range(nb):
-        table[my_g, b, my_rows, :] = plus[me * nb + b]
+        table[my_g, b, my_rows, :] = plus[my_f, my_g, b]
+    if paired:
+        away = 1 - home
+        away_rows = pl.ds(pl.multiple_of(away * group, group), group)
+
+        @pl.when(straight)
+        def _():
+            mirror[...] = jnp.zeros_like(mirror)
+
+        @pl.when(crossed)
+        def _():
+            table[home, :, away_rows, :] = jnp.zeros((nb, group, col_count), jnp.float32)
+            minus[...] = (raw[0] - raw[1]).reshape(minus.shape)
+            for b in range(nb):
+                mirror[b, near_rows, :] = minus[my_f, my_g, b]
+
+    if modes < LANES:
+        shapes[:, :, modes:, :] = jnp.zeros((ng, nb, LANES - modes, col_count), jnp.float32)
 
     for copy in owned:
         copy.wait()
@@ -129,7 +159,7 @@
     def mode_copies(k):
         peer = lax.rem(my_g + k, ng)
         theirs = pl.ds(peer * nb, nb)
-        places = (shapes.at[my_g], sources.at[my_g, :, 0:modes, :])
+        places = (shapes.at[my_g, :, 0:modes, :], sources.at[my_g, :, 0:modes, :])
         return [
             pltpu.make_async_remote_copy(
                 src_ref=modes_out.at[i, theirs],
@@ -142,32 +172,101 @@
             for i, here in enumerate(places)
         ]
 
-    for k in range(1, ng):
-        for copy in mode_copies(k):
-            copy.start()
-
-    def piece(f, g):
+    def copy_to(source, target, i, f, g):
         return pltpu.make_async_remote_copy(
-            src_ref=plus.at[pl.ds((f * ng + g) * nb, nb)],
-            dst_ref=table.at[my_g, :, my_rows, :],
-            send_sem=send_sem,
-            recv_sem=recv_sem,
+            src_ref=source,
+            dst_ref=target,
+            send_sem=send_sem.at[i],
+            recv_sem=recv_sem.at[i],
             device_id=(f, g),
             device_id_type=MESH,
         )
 
-    def send_plane(shift):
-        for j in range(span * ng - 1, -1, -1):
-            if j > 0 or shift is not None:
+    last = away * (nf - span) if paired else 0
+
+    def relay_copy():
+        return pltpu.make_async_remote_copy(
+            src_ref=plus.at[pl.ds(last, span), 1 - my_g],
+            dst_ref=relay,
+            send_sem=relay_send,
+            recv_sem=relay_recv,
+            device_id=(my_f, 1 - my_g),
+            device_id_type=MESH,
+        )
+
+    def send_near(shift, start):
+        peers = [(j, flipped(j)) for j in range(span * ng - 1, start - 1, -1)]
+        for j, (f, g) in peers:
+            f = f + shift
+            copy_to(plus.at[f, g], table.at[my_g, :, my_rows, :], 0, f, g).start()
+        if paired:
+
+            @pl.when(crossed)
+            def _():
+                for j, (f, g) in peers:
+                    if j % ng == 0:
+                        f = f + shift
+                        copy_to(minus.at[f, g], mirror.at[:, near_rows, :], 1, f, g).start()
+
+    def send_far(shift, straight_only, crossed_only):
+        ends = (my_f + shift) // span * span == last
+        target = table.at[home, :, my_rows, :]
+
+        def sends(source, js):
+            for j in js:
                 f, g = flipped(j)
-                piece(f if shift is None else f + shift, g).start()
-
-    send_plane(None)
-    for k in range(PLANES - 1, 0, -1):
-
-        @pl.when(plane >= k)
-        def _():
-            send_plane(-k * span)
+                f = f + shift
+                copy_to(source(f, g), target, 0, f, g).start()
+
+        if not crossed_only:
+
+            @pl.when(straight & jnp.logical_not(ends))
+            def _():
+                sends(lambda f, g: plus.at[f, g], range(span * ng - 1, -1, -1))
+
+            @pl.when(straight & ends)
+            def _():
+                sends(lambda f, g: plus.at[f, g], range((span - 1) * ng, -1, -ng))
+
+        if straight_only or not crossed_only:
+
+            @pl.when(crossed)
+            def _():
+                for j in range((span - 1) * ng, -1, -ng):
+                    f = flipped(j)[0] + shift
+                    copy_to(plus.at[f, my_g], table.at[my_g, :, my_rows, :], 0, f, my_g).start()
+
+        if not straight_only:
+
+            @pl.when(crossed & ends)
+            def _():
+                sends(lambda f, g: relay.at[f - last], range((span - 1) * ng, -1, -ng))
+
+    def send_plane(shift, **which):
+        if not paired:
+            send_near(shift, 0)
+            return
+        there = (my_f + shift) // per
+
+        @pl.when(there == home)
+        def _():
+            send_near(shift, 0)
+
+        @pl.when(there != home)
+        def _():
+            send_far(shift, **which)
+
+    if paired:
+
+        @pl.when(straight)
+        def _():
+            relay_copy().start()
+
+    @pl.when(plane > 0)
+    def _():
+        for k in range(1, ng):
+            for copy in mode_copies(k):
+                copy.start()
 
     for copy in small:
         copy.wait()
@@ -207,12 +306,42 @@
             first[b, d] = one
             second[b, d] = two
 
+    send_near(0, 1)
+    for k in range(PLANES - 1, 0, -1):
+
+        @pl.when(plane >= k)
+        def _():
+            send_plane(-k * span, straight_only=True, crossed_only=False)
+
+    if paired:
+
+        @pl.when(crossed & (plane >= PLANES // 2))
+        def _():
+            relay_copy().wait_recv()
+            for k in range(PLANES // 2, PLANES):
+
+                @pl.when(plane == k)
+                def _():
+                    send_far(-k * span, False, True)
+
     for k in range(1, PLANES):
 
         @pl.when(plane + k < PLANES)
         def _():
             pl.semaphore_wait(known.at[plane + k], 1)
-            send_plane(k * span)
+            if paired:
+
+                @pl.when(crossed & (plane < PLANES // 2) & (plane + k == PLANES - 1))
+                def _():
+                    relay_copy().wait_recv()
+
+            send_plane(k * span, straight_only=False, crossed_only=False)
+
+    @pl.when(plane == 0)
+    def _():
+        for k in range(1, ng):
+            for copy in mode_copies(k):
+                copy.start()
 
     def lay_products(b, g):
         here = sources[g, b, 0:modes, :]
@@ -230,11 +359,8 @@
         for copy in mode_copies(k):
             copy.wait_recv()
 
-    wide[...] = jnp.zeros_like(wide)
     for b in range(nb):
         for g in range(ng):
-            wide[b, 0:modes, g * col_count : (g + 1) * col_count] = shapes[g, b]
-
             @pl.when(my_g != g)
             def _():
                 sources[g, b, modes : 2 * modes, :] = sources[g, b, 0:modes, :]
@@ -260,30 +386,46 @@
         return jnp.broadcast_to(ref[d : d + 1, :], (ranges, LANES))
 
     for b in range(nb):
+        wide = jnp.concatenate([shapes[g, b] for g in range(ng)], axis=1)
         gram = lax.dot_general(
-            wide[b, 0:modes], wide[b], NT, precision=HIGH, preferred_element_type=jnp.float32
+            wide[0:modes], wide, NT, precision=HIGH, preferred_element_type=jnp.float32
         )
         rows[0:modes, :] = diagonals(gram, modes)
         value = forms(b, lambda d: spread(rows, d) * (first[b, d] + second[b, d]))
-        denom[b] = value * float(bins)
+        denom[b] = value * float(devices * nb)
 
     def settle(ref, sem):
         pltpu.make_async_copy(ref, ref, sem).wait()
 
-    settle(plus.at[pl.ds(0, (devices - 1) * nb)], recv_sem)
+    def pieces(count):
+        return raw.at[0, pl.ds(0, count * nb)]
+
+    if paired:
+
+        @pl.when(straight)
+        def _():
+            settle(pieces(devices - 1), recv_sem.at[0])
+
+        @pl.when(crossed)
+        def _():
+            settle(pieces(nf + per - 1), recv_sem.at[0])
+            settle(pieces(per - 1), recv_sem.at[1])
+
+    else:
+        settle(pieces(devices - 1), recv_sem.at[0])
 
     for b in range(nb):
-        left_high, left_low = split(wide[b])
-        whole = jnp.concatenate([table[g, b] for g in range(ng)], axis=1)
-        mid_high, mid_low = split(whole)
-        high, low = left_high[0:modes], left_low[0:modes]
-        both = product(jnp.concatenate([high, low], 0), mid_high, NN)
-        middle = both[:modes] + (both[modes:] + product(high, mid_low, NN))
-        half_high, half_low = split(middle)
-        both = product(jnp.concatenate([half_high, half_low], 0), left_high, NT)
-        forward = both[:modes] + (both[modes:] + product(half_high, left_low, NT))
+        blocks = [split(shapes[g, b]) for g in range(ng)]
+        left = [jnp.concatenate([block[i] for block in blocks], axis=1) for i in range(2)]
+        whole = split(jnp.concatenate([table[g, b] for g in range(ng)], axis=1))
+        both = thrice(split(thrice(left, whole, modes, NN)), left, modes, NT)
         square = jnp.zeros((LANES - modes, LANES), jnp.float32)
-        backward = jnp.concatenate([forward, square], 0).T[0:modes]
+        forward, backward = both, jnp.concatenate([both, square], 0).T[0:modes]
+        if paired:
+            here, there = split(shapes[home, b]), split(shapes[away, b])
+            across = thrice(split(thrice(here, split(mirror[b]), modes, NN)), there, modes, NT)
+            backward = backward + across
+            forward = forward + jnp.concatenate([across, square], 0).T[0:modes]
         rows[0:modes, :] = diagonals(backward, modes)
         rows[LANES : LANES + modes, :] = diagonals(forward, modes)
 
@@ -314,7 +456,20 @@
         for copy in mode_copies(k):
             copy.wait_send()
 
-    settle(plus.at[pl.ds(0, (devices - 1) * nb)], send_sem)
+    if paired:
+        settle(pieces(nf - 1 + nf - span), send_sem.at[0])
+
+        @pl.when(crossed)
+        def _():
+            settle(pieces(per - 1), send_sem.at[1])
+
+        @pl.when(straight)
+        def _():
+            relay_copy().wait_send()
+
+    else:
+        settle(pieces(devices - 1), send_sem.at[0])
+
     settle(parts.at[pl.ds(0, devices - 1)], part_send)
     settle(parts.at[pl.ds(0, devices - 1)], part_recv)
     out_ref[...] = jnp.sum(parts[...], axis=0)
@@ -347,12 +502,14 @@
                 pltpu.VMEM((bins_here, modes), f32),
                 pltpu.SMEM((bins_here,), jnp.int32),
                 pltpu.VMEM((two, bins, rows, cols), f32),
-                pltpu.VMEM((bins, rows, cols), f32),
+                pltpu.VMEM((nf, ng, nb, rows, cols), f32),
+                pltpu.VMEM((nf, ng, nb, rows, cols), f32),
                 pltpu.VMEM((ng, nb, nf * rows, cols), f32),
+                pltpu.VMEM((nb, nf // ng * rows, cols), f32),
+                pltpu.VMEM((nf // PLANES, nb, rows, cols), f32),
                 pltpu.VMEM((2, bins_here, modes, cols), f32),
-                pltpu.VMEM((ng, nb, modes, cols), f32),
+                pltpu.VMEM((ng, nb, LANES, cols), f32),
                 pltpu.VMEM((ng, nb, 2 * modes, depth_here), f32),
-                pltpu.VMEM((nb, LANES, ng * cols), f32),
                 pltpu.VMEM((nb, modes // 2 + 1, ranges, LANES), f32),
                 pltpu.VMEM((nb, modes // 2 + 1, ranges, LANES), f32),
                 pltpu.VMEM((nb, ng, slots * LANES, depth_here), bf16),
@@ -362,7 +519,7 @@
                 pltpu.VMEM((devices, share, depth_here), f32),
                 pltpu.SemaphoreType.REGULAR((PLANES,)),
                 dma((3,)), dma, dma((5,)), dma((2, max(ng - 1, 1))), dma((2, max(ng - 1, 1))),
-                dma, dma, dma, dma,
+                dma((2,)), dma((2,)), dma, dma, dma, dma,
             ],
             compiler_params=pltpu.CompilerParams(
                 collective_id=0, has_side_effects=True, vmem_limit_bytes=32 * 1024 * 1024

time: 20.9 us -> 19.8 us (0.947)
  Pallas kernels: 20.2 us -> 19 us
    pallas_call x1, Pallas kernels: 20.2 us -> 19 us  [per_device(): pl.pallas_call(functools.partial(kernel, nf, ng), out_shape=jax.ShapeDtyp...]
where the time goes in v3:
time: 19.8 us; the launch traced here: 19.6 us
  Pallas kernels  19 us (96%)
  local copies, waits for them, and re-layouts  0.58 us (3%)
    pallas_call x1, Pallas kernels, per_device(): pl.pallas_call(functools.partial(kernel, nf, ng), out_shape=jax.ShapeDtyp...  19 us
    unnamed x1, local copies, waits for them, and re-layouts  0.58 us

profile of v3, /device:TPU:0, one launch (start us, length us, event | category | flops | bytes accessed | tf_op | source)
XLA Modules:
  0.0 19.6 jit_solution(9928680649451088104)
XLA Ops:
  0.0 19.0 %shard_map.64 = f32[4,128]{1,0:T(4,128)S(1)} custom-call(f32[2,32,16,128]{3,2,1,0:T(8,128)} %spectra_hbm.1, f32[2,96,128]{2,1,0:T(8,128)} %sensor_hbm.1, f32[2,96,128]{2,1,0:T(8,128)} %source_hbm.1, f32[2,96]{1,0:T(2,128)} %wave_hbm.1, f32[2,96]{1,0:T(2,128)} %atten_hbm.1, s32[2]{0:T(128)} %counts_hbm.1), custom_call_target="tpu_custom_call" | custom-call | tf_op jit(solution)/shard_map/pallas_call | solution.py:495
  19.0 0.6 %copy.8 = f32[4,128]{1,0:T(4,128)} copy(f32[4,128]{1,0:T(4,128)S(1)} %shard_map.64) | data formatting | bytes 4096

commit v4 on v3

--- a/solution.py
+++ b/solution.py
@@ -103,6 +103,9 @@
     for j in range(span * ng - 1, 0, -1):
         signal(barrier, *flipped(j))
 
+    def settle(ref, sem):
+        pltpu.make_async_copy(ref, ref, sem).wait()
+
     raw_copy = pltpu.make_async_copy(spectra_hbm, raw, raw_sem)
     raw_copy.start()
     small = [
@@ -112,13 +115,12 @@
     own = pl.ds(my_g * nb, nb)
     owned = [
         pltpu.make_async_copy(hbm, here, own_sem.at[i])
-        for i, (hbm, here) in enumerate((
-            (sensor_hbm, modes_out.at[0]),
-            (source_hbm, modes_out.at[1]),
-            (sensor_hbm.at[own], shapes.at[my_g, :, 0:modes, :]),
-            (source_hbm.at[own], sources.at[my_g, :, 0:modes, :]),
-            (source_hbm.at[own], sources.at[my_g, :, modes : 2 * modes, :]),
-        ))
+        for i, hbm, here in (
+            (0, sensor_hbm, modes_out.at[0]),
+            (0, source_hbm, modes_out.at[1]),
+            (1, source_hbm.at[own], sources.at[my_g, :, 0:modes, :]),
+            (1, source_hbm.at[own], sources.at[my_g, :, modes : 2 * modes, :]),
+        )
     ]
     for copy in small + owned:
         copy.start()
@@ -147,8 +149,10 @@
     if modes < LANES:
         shapes[:, :, modes:, :] = jnp.zeros((ng, nb, LANES - modes, col_count), jnp.float32)
 
-    for copy in owned:
-        copy.wait()
+    settle(modes_out, own_sem.at[0])
+    settle(sources.at[my_g], own_sem.at[1])
+    for b in range(nb):
+        shapes[my_g, b, 0:modes, :] = modes_out[0, my_g * nb + b]
     pl.semaphore_wait(barrier, (plane + 1) * span * ng - 1)
     for k in range(PLANES - 1, 0, -1):
 
@@ -164,8 +168,8 @@
             pltpu.make_async_remote_copy(
                 src_ref=modes_out.at[i, theirs],
                 dst_ref=here,
-                send_sem=mode_send.at[i, k - 1],
-                recv_sem=mode_recv.at[i, k - 1],
+                send_sem=mode_send.at[k - 1],
+                recv_sem=mode_recv.at[k - 1],
                 device_id=(my_f, peer),
                 device_id_type=MESH,
             )
@@ -228,19 +232,22 @@
             def _():
                 sends(lambda f, g: plus.at[f, g], range((span - 1) * ng, -1, -ng))
 
-        if straight_only or not crossed_only:
-
-            @pl.when(crossed)
-            def _():
-                for j in range((span - 1) * ng, -1, -ng):
-                    f = flipped(j)[0] + shift
+        def crossing(direct, forward):
+            base = (my_f + shift) // span * span
+            for o in sorted(range(span), key=lambda o: (-(o // 2), o)):
+                f = base + o
+                if direct:
                     copy_to(plus.at[f, my_g], table.at[my_g, :, my_rows, :], 0, f, my_g).start()
-
-        if not straight_only:
-
-            @pl.when(crossed & ends)
-            def _():
-                sends(lambda f, g: relay.at[f - last], range((span - 1) * ng, -1, -ng))
+                if forward:
+                    copy_to(relay.at[f - last], target, 0, f, my_g).start()
+
+        if straight_only:
+            pl.when(crossed)(lambda: crossing(True, False))
+        elif crossed_only:
+            pl.when(crossed & ends)(lambda: crossing(False, True))
+        else:
+            pl.when(crossed & ends)(lambda: crossing(True, True))
+            pl.when(crossed & jnp.logical_not(ends))(lambda: crossing(True, False))
 
     def send_plane(shift, **which):
         if not paired:
@@ -356,8 +363,7 @@
                     right[b, g, slot * LANES + modes : (slot + 1) * LANES, :] = none
 
     for k in range(1, ng):
-        for copy in mode_copies(k):
-            copy.wait_recv()
+        settle(modes_out.at[:, pl.ds(0, nb)], mode_recv.at[k - 1])
 
     for b in range(nb):
         for g in range(ng):
@@ -367,23 +373,24 @@
 
             lay_products(b, g)
 
-    def forms(b, lefts):
+    def slots_of(lefts):
         slots = []
         for d in range(half + 1):
-            value = lefts(d)
-            high, low = split(value)
+            high, low = split(lefts(d))
             slots += [high, low, high] if d == 0 else [high]
-        totals = [None] * ng
+        return slots
+
+    def form(b, g, slots):
+        total = None
         for k in range(0, len(slots), CHUNK):
             left = jnp.concatenate(slots[k : k + CHUNK], axis=1)
             end = k + len(slots[k : k + CHUNK])
-            for n in range(ng):
-                part = product(left, right[b, n, k * LANES : end * LANES, :], NN)
-                totals[n] = part if totals[n] is None else totals[n] + part
-        return jnp.concatenate(totals, axis=1)
-
-    def spread(ref, d):
-        return jnp.broadcast_to(ref[d : d + 1, :], (ranges, LANES))
+            part = product(left, right[b, g, k * LANES : end * LANES, :], NN)
+            total = part if total is None else total + part
+        return total
+
+    def spread(ref, d, count):
+        return jnp.broadcast_to(ref[d : d + 1, :], (count, LANES))
 
     for b in range(nb):
         wide = jnp.concatenate([shapes[g, b] for g in range(ng)], axis=1)
@@ -391,11 +398,9 @@
             wide[0:modes], wide, NT, precision=HIGH, preferred_element_type=jnp.float32
         )
         rows[0:modes, :] = diagonals(gram, modes)
-        value = forms(b, lambda d: spread(rows, d) * (first[b, d] + second[b, d]))
-        denom[b] = value * float(devices * nb)
-
-    def settle(ref, sem):
-        pltpu.make_async_copy(ref, ref, sem).wait()
+        slots = slots_of(lambda d: spread(rows, d, ranges) * (first[b, d] + second[b, d]))
+        for g in range(ng):
+            denom[b, g] = form(b, g, slots) * float(devices * nb)
 
     def pieces(count):
         return raw.at[0, pl.ds(0, count * nb)]
@@ -413,30 +418,6 @@
 
     else:
         settle(pieces(devices - 1), recv_sem.at[0])
-
-    for b in range(nb):
-        blocks = [split(shapes[g, b]) for g in range(ng)]
-        left = [jnp.concatenate([block[i] for block in blocks], axis=1) for i in range(2)]
-        whole = split(jnp.concatenate([table[g, b] for g in range(ng)], axis=1))
-        both = thrice(split(thrice(left, whole, modes, NN)), left, modes, NT)
-        square = jnp.zeros((LANES - modes, LANES), jnp.float32)
-        forward, backward = both, jnp.concatenate([both, square], 0).T[0:modes]
-        if paired:
-            here, there = split(shapes[home, b]), split(shapes[away, b])
-            across = thrice(split(thrice(here, split(mirror[b]), modes, NN)), there, modes, NT)
-            backward = backward + across
-            forward = forward + jnp.concatenate([across, square], 0).T[0:modes]
-        rows[0:modes, :] = diagonals(backward, modes)
-        rows[LANES : LANES + modes, :] = diagonals(forward, modes)
-
-        def left(d):
-            return spread(rows, d) * first[b, d] + spread(rows, LANES + d) * second[b, d]
-
-        score = forms(b, left) / denom[b]
-        for g in range(ng):
-            at = slice(g * depth_here, (g + 1) * depth_here)
-            value = score[:, at].reshape(nf, share, depth_here)
-            power[g] = value if b == 0 else power[g] + value
 
     def part(f, g):
         return pltpu.make_async_remote_copy(
@@ -448,13 +429,82 @@
             device_id_type=MESH,
         )
 
+    head = max(span * share, 16)
+    for b in range(nb):
+        blocks = [split(shapes[g, b]) for g in range(ng)]
+        left = [jnp.concatenate([block[i] for block in blocks], axis=1) for i in range(2)]
+
+        def projected():
+            whole = split(jnp.concatenate([table[g, b] for g in range(ng)], axis=1))
+            return thrice(split(thrice(left, whole, modes, NN)), left, modes, NT)
+
+        square = jnp.zeros((LANES - modes, LANES), jnp.float32)
+
+        def turned(value):
+            return jnp.concatenate([value, square], 0).T[0:modes]
+
+        def lay(forward, backward):
+            rows[0:modes, :] = diagonals(backward, modes)
+            rows[LANES : LANES + modes, :] = diagonals(forward, modes)
+
+        if paired:
+
+            @pl.when(straight)
+            def _():
+                both = projected()
+                lay(both, turned(both))
+
+            @pl.when(crossed)
+            def _():
+                both = projected()
+                here, there = split(shapes[home, b]), split(shapes[away, b])
+                across = thrice(split(thrice(here, split(mirror[b]), modes, NN)), there, modes, NT)
+                lay(both + turned(across), turned(both) + across)
+
+        else:
+            both = projected()
+            lay(both, turned(both))
+
+        def slots_at(low, high):
+            count = high - low
+            return slots_of(
+                lambda d: spread(rows, d, count) * first[b, d, low:high, :]
+                + spread(rows, LANES + d, count) * second[b, d, low:high, :]
+            )
+
+        def place(g, low, score):
+            score = score / denom[b, g, low : low + score.shape[0], :]
+            at = slice(low // share, (low + score.shape[0]) // share)
+            value = score.reshape(at.stop - at.start, share, depth_here)
+            power[g, at] = value if b == 0 else power[g, at] + value
+
+        early = slots_at(0, head)
+        place(0, 0, form(b, 0, early))
+        if b == nb - 1:
+            for f in range(head // share):
+
+                @pl.when(me != f * ng)
+                def _():
+                    part(jnp.int32(f), jnp.int32(0)).start()
+
+        late = slots_at(head, ranges)
+        if head < ranges:
+            place(0, head, form(b, 0, late))
+        every = [jnp.concatenate(pair, 0) for pair in zip(early, late)]
+        for g in range(1, ng):
+            place(g, 0, form(b, g, every))
+
     for j in range(devices - 1, 0, -1):
-        part(*flipped(j)).start()
+        f, g = flipped(j)
+
+        @pl.when((f >= head // share) | (g > 0))
+        def _():
+            part(f, g).start()
+
     parts[me] = power[my_g, my_f]
 
     for k in range(1, ng):
-        for copy in mode_copies(k):
-            copy.wait_send()
+        settle(modes_out.at[:, pl.ds(0, nb)], mode_send.at[k - 1])
 
     if paired:
         settle(pieces(nf - 1 + nf - span), send_sem.at[0])
@@ -514,11 +564,11 @@
                 pltpu.VMEM((nb, modes // 2 + 1, ranges, LANES), f32),
                 pltpu.VMEM((nb, ng, slots * LANES, depth_here), bf16),
                 pltpu.VMEM((2 * LANES, LANES), f32),
-                pltpu.VMEM((nb, ranges, ng * depth_here), f32),
+                pltpu.VMEM((nb, ng, ranges, depth_here), f32),
                 pltpu.VMEM((ng, nf, share, depth_here), f32),
                 pltpu.VMEM((devices, share, depth_here), f32),
                 pltpu.SemaphoreType.REGULAR((PLANES,)),
-                dma((3,)), dma, dma((5,)), dma((2, max(ng - 1, 1))), dma((2, max(ng - 1, 1))),
+                dma((3,)), dma, dma((2,)), dma((max(ng - 1, 1),)), dma((max(ng - 1, 1),)),
                 dma((2,)), dma((2,)), dma, dma, dma, dma,
             ],
             compiler_params=pltpu.CompilerParams(

time: 19.8 us -> 19.1 us (0.965)
  Pallas kernels: 19 us -> 18.4 us
    pallas_call x1, Pallas kernels: 19 us -> 18.4 us  [per_device(): pl.pallas_call(functools.partial(kernel, nf, ng), out_shape=jax.ShapeDtyp...]
where the time goes in v4:
time: 19.1 us; the launch traced here: 19 us
  Pallas kernels  18.4 us (96%)
  local copies, waits for them, and re-layouts  0.58 us (3%)
    pallas_call x1, Pallas kernels, per_device(): pl.pallas_call(functools.partial(kernel, nf, ng), out_shape=jax.ShapeDtyp...  18.4 us
    unnamed x1, local copies, waits for them, and re-layouts  0.58 us

profile of v4, /device:TPU:0, one launch (start us, length us, event | category | flops | bytes accessed | tf_op | source)
XLA Modules:
  0.0 19.0 jit_solution(11510046310842351673)
XLA Ops:
  0.0 18.4 %shard_map.64 = f32[4,128]{1,0:T(4,128)S(1)} custom-call(f32[2,32,16,128]{3,2,1,0:T(8,128)} %spectra_hbm.1, f32[2,96,128]{2,1,0:T(8,128)} %sensor_hbm.1, f32[2,96,128]{2,1,0:T(8,128)} %source_hbm.1, f32[2,96]{1,0:T(2,128)} %wave_hbm.1, f32[2,96]{1,0:T(2,128)} %atten_hbm.1, s32[2]{0:T(128)} %counts_hbm.1), custom_call_target="tpu_custom_call" | custom-call | tf_op jit(solution)/shard_map/pallas_call | solution.py:545
  18.4 0.6 %copy.8 = f32[4,128]{1,0:T(4,128)} copy(f32[4,128]{1,0:T(4,128)S(1)} %shard_map.64) | data formatting | bytes 4096

commit v5 on v4

--- a/solution.py
+++ b/solution.py
@@ -216,25 +216,21 @@
         ends = (my_f + shift) // span * span == last
         target = table.at[home, :, my_rows, :]
 
-        def sends(source, js):
-            for j in js:
-                f, g = flipped(j)
-                f = f + shift
-                copy_to(source(f, g), target, 0, f, g).start()
+        base = (my_f + shift) // span * span
+        order = sorted(range(span), key=lambda o: (-(o // 2), o))
+
+        def sends(grids):
+            for o in order:
+                for g in grids:
+                    f = base + o
+                    copy_to(plus.at[f, g], target, 0, f, g).start()
 
         if not crossed_only:
-
-            @pl.when(straight & jnp.logical_not(ends))
-            def _():
-                sends(lambda f, g: plus.at[f, g], range(span * ng - 1, -1, -1))
-
-            @pl.when(straight & ends)
-            def _():
-                sends(lambda f, g: plus.at[f, g], range((span - 1) * ng, -1, -ng))
+            pl.when(straight & jnp.logical_not(ends))(lambda: sends((1 - my_g, my_g)))
+            pl.when(straight & ends)(lambda: sends((my_g,)))
 
         def crossing(direct, forward):
-            base = (my_f + shift) // span * span
-            for o in sorted(range(span), key=lambda o: (-(o // 2), o)):
+            for o in order:
                 f = base + o
                 if direct:
                     copy_to(plus.at[f, my_g], table.at[my_g, :, my_rows, :], 0, f, my_g).start()
@@ -274,6 +270,15 @@
         for k in range(1, ng):
             for copy in mode_copies(k):
                 copy.start()
+
+    @pl.when(plane == PLANES - 1)
+    def _():
+        send_near(0, 1)
+        for k in range(PLANES - 1, 0, -1):
+
+            @pl.when(plane >= k)
+            def _():
+                send_plane(-k * span, straight_only=True, crossed_only=False)
 
     for copy in small:
         copy.wait()
@@ -313,12 +318,14 @@
             first[b, d] = one
             second[b, d] = two
 
-    send_near(0, 1)
-    for k in range(PLANES - 1, 0, -1):
-
-        @pl.when(plane >= k)
-        def _():
-            send_plane(-k * span, straight_only=True, crossed_only=False)
+    @pl.when(plane < PLANES - 1)
+    def _():
+        send_near(0, 1)
+        for k in range(PLANES - 1, 0, -1):
+
+            @pl.when(plane >= k)
+            def _():
+                send_plane(-k * span, straight_only=True, crossed_only=False)
 
     if paired:
 

time: 19.1 us -> 19.1 us (level)
  no operation moved by 1% of the time
where the time goes in v5:
time: 19.1 us; the launch traced here: 18.9 us
  Pallas kernels  18.4 us (96%)
  local copies, waits for them, and re-layouts  0.58 us (3%)
    pallas_call x1, Pallas kernels, per_device(): pl.pallas_call(functools.partial(kernel, nf, ng), out_shape=jax.ShapeDtyp...  18.4 us
    unnamed x1, local copies, waits for them, and re-layouts  0.58 us

profile of v5, /device:TPU:0, one launch (start us, length us, event | category | flops | bytes accessed | tf_op | source)
XLA Modules:
  0.0 18.9 jit_solution(13096060422142876905)
XLA Ops:
  0.0 18.4 %shard_map.64 = f32[4,128]{1,0:T(4,128)S(1)} custom-call(f32[2,32,16,128]{3,2,1,0:T(8,128)} %spectra_hbm.1, f32[2,96,128]{2,1,0:T(8,128)} %sensor_hbm.1, f32[2,96,128]{2,1,0:T(8,128)} %source_hbm.1, f32[2,96]{1,0:T(2,128)} %wave_hbm.1, f32[2,96]{1,0:T(2,128)} %atten_hbm.1, s32[2]{0:T(128)} %counts_hbm.1), custom_call_target="tpu_custom_call" | custom-call | tf_op jit(solution)/shard_map/pallas_call | solution.py:552
  18.4 0.6 %copy.8 = f32[4,128]{1,0:T(4,128)} copy(f32[4,128]{1,0:T(4,128)S(1)} %shard_map.64) | data formatting | bytes 4096

commit v6 on v5

--- a/solution.py
+++ b/solution.py
@@ -47,7 +47,7 @@
     nf, ng,
     spectra_hbm, sensor_hbm, source_hbm, wave_hbm, atten_hbm, counts_hbm,
     out_ref,
-    wave, atten, counts, raw, plus, minus, table, mirror, relay, modes_out, shapes, sources,
+    tables, counts, raw, plus, minus, table, mirror, relay, modes_out, shapes, sources,
     first, second, right, rows, denom, power, parts,
     known, small_sem, raw_sem, own_sem, mode_send, mode_recv, send_sem, recv_sem,
     relay_send, relay_recv, part_send, part_recv,
@@ -110,7 +110,7 @@
     raw_copy.start()
     small = [
         pltpu.make_async_copy(hbm, here, small_sem.at[i])
-        for i, (hbm, here) in enumerate(((wave_hbm, wave), (atten_hbm, atten), (counts_hbm, counts)))
+        for i, hbm, here in (((0, wave_hbm, tables.at[0]), (0, atten_hbm, tables.at[1]), (1, counts_hbm, counts)))
     ]
     own = pl.ds(my_g * nb, nb)
     owned = [
@@ -158,7 +158,7 @@
 
         @pl.when(plane >= k)
         def _():
-            signal(known.at[plane], my_f - k * span, my_g)
+            signal(known.at[plane - 1], my_f - k * span, my_g)
 
     def mode_copies(k):
         peer = lax.rem(my_g + k, ng)
@@ -280,15 +280,15 @@
             def _():
                 send_plane(-k * span, straight_only=True, crossed_only=False)
 
-    for copy in small:
-        copy.wait()
+    settle(tables, small_sem.at[0])
+    small[2].wait()
     radius = 1.0 + lax.broadcasted_iota(jnp.int32, (ranges, LANES), 0).astype(jnp.float32)
     lane = lax.broadcasted_iota(jnp.int32, (ranges, LANES), 1)
     for b in range(nb):
         row = my_g * nb + b
         rows[...] = jnp.ones_like(rows)
-        rows[0:1, 0:modes] = wave[pl.ds(row, 1), :]
-        rows[1:2, 0:modes] = atten[pl.ds(row, 1), :]
+        rows[0:1, 0:modes] = tables[0, pl.ds(row, 1), :]
+        rows[1:2, 0:modes] = tables[1, pl.ds(row, 1), :]
         phase = radius * rows[0:1, :]
         magnitude = jnp.exp(-rows[1:2, :] * radius) / jnp.sqrt(phase)
         magnitude = jnp.where(lane < jnp.minimum(counts[row], modes), magnitude, 0.0)
@@ -342,7 +342,7 @@
 
         @pl.when(plane + k < PLANES)
         def _():
-            pl.semaphore_wait(known.at[plane + k], 1)
+            pl.semaphore_wait(known.at[plane + k - 1], 1)
             if paired:
 
                 @pl.when(crossed & (plane < PLANES // 2) & (plane + k == PLANES - 1))
@@ -555,8 +555,7 @@
             in_specs=[pl.BlockSpec(memory_space=pltpu.HBM)] * 6,
             out_specs=pl.BlockSpec(memory_space=pltpu.VMEM),
             scratch_shapes=[
-                pltpu.VMEM((bins_here, modes), f32),
-                pltpu.VMEM((bins_here, modes), f32),
+                pltpu.VMEM((2, bins_here, modes), f32),
                 pltpu.SMEM((bins_here,), jnp.int32),
                 pltpu.VMEM((two, bins, rows, cols), f32),
                 pltpu.VMEM((nf, ng, nb, rows, cols), f32),
@@ -574,8 +573,8 @@
                 pltpu.VMEM((nb, ng, ranges, depth_here), f32),
                 pltpu.VMEM((ng, nf, share, depth_here), f32),
                 pltpu.VMEM((devices, share, depth_here), f32),
-                pltpu.SemaphoreType.REGULAR((PLANES,)),
-                dma((3,)), dma, dma((2,)), dma((max(ng - 1, 1),)), dma((max(ng - 1, 1),)),
+                pltpu.SemaphoreType.REGULAR((PLANES - 1,)),
+                dma((2,)), dma, dma((2,)), dma((max(ng - 1, 1),)), dma((max(ng - 1, 1),)),
                 dma((2,)), dma((2,)), dma, dma, dma, dma,
             ],
             compiler_params=pltpu.CompilerParams(

time: 19.1 us -> 19.1 us (level)
  no operation moved by 1% of the time
where the time goes in v6:
time: 19.1 us; the launch traced here: 18.9 us
  Pallas kernels  18.3 us (96%)
  local copies, waits for them, and re-layouts  0.58 us (3%)
    pallas_call x1, Pallas kernels, per_device(): pl.pallas_call(functools.partial(kernel, nf, ng), out_shape=jax.ShapeDtyp...  18.3 us
    unnamed x1, local copies, waits for them, and re-layouts  0.58 us

profile of v6, /device:TPU:0, one launch (start us, length us, event | category | flops | bytes accessed | tf_op | source)
XLA Modules:
  0.0 18.9 jit_solution(3586217116823388834)
XLA Ops:
  0.0 18.3 %shard_map.64 = f32[4,128]{1,0:T(4,128)S(1)} custom-call(f32[2,32,16,128]{3,2,1,0:T(8,128)} %spectra_hbm.1, f32[2,96,128]{2,1,0:T(8,128)} %sensor_hbm.1, f32[2,96,128]{2,1,0:T(8,128)} %source_hbm.1, f32[2,96]{1,0:T(2,128)} %wave_hbm.1, f32[2,96]{1,0:T(2,128)} %atten_hbm.1, s32[2]{0:T(128)} %counts_hbm.1), custom_call_target="tpu_custom_call" | custom-call | tf_op jit(solution)/shard_map/pallas_call | solution.py:552
  18.3 0.6 %copy.8 = f32[4,128]{1,0:T(4,128)} copy(f32[4,128]{1,0:T(4,128)S(1)} %shard_map.64) | data formatting | bytes 4096
